TPU v7x, 32 devices: a whole 2x2x4 slice. The times are simulated.
32 devices in a mesh: row: 4 (over y, x), col: 4 (over z), dep: 2 (over core).
Axes of the slice: x: 2, y: 2, z: 4, core: 2. Of those that a mesh axis runs over, the one named last changes fastest.
Arguments:
- matrix: float32 [16384, 16384], P('row', ('col', 'dep')), may hold values from -6 to 6
- vectors: float32 [64, 16384], P(None, ('row', 'col')), may hold values from -0.09375 to 0.09375
Outputs:
- reduced: float32 [16384, 16384], P('row', ('col', 'dep'))
All inputs are finite; a program needn't handle non-finite values.
Results may differ from a plain program's by a relative error of at most 0.0001.
Values sent between devices are 32-bit elements; how exact they have to be, the bound alone decides.
A program may use at most 128 MiB of HBM per device.

v0:
```python
import jax
import jax.numpy as jnp
from jax import lax
from jax.sharding import PartitionSpec as P

highest = lax.Precision.HIGHEST


def broadcast(value, axis, source):
    kept = jnp.where(lax.axis_index(axis) == source, value, 0).astype(value.dtype)
    return lax.psum(kept, axis)


def contract(left, right, dims):
    return lax.dot_general(left, right, (dims, ((), ())), precision=highest)


def mask_vectors(values, first_row):
    panel_width, row_count = values.shape
    positions = first_row + lax.iota(jnp.int32, row_count)[None, :]
    reflector = lax.iota(jnp.int32, panel_width)[:, None]
    filler = jnp.where(positions == reflector + 1, 1.0, 0.0).astype(values.dtype)
    return jnp.where(positions > reflector + 1, values, filler)


def make_factor(gram):
    size_b = gram.shape[0]
    half_diag = 0.5 * jnp.diagonal(gram)
    scaled = jnp.triu(gram, 1) / half_diag[:, None]
    identity = jnp.eye(size_b, dtype=gram.dtype)
    inverse = identity - scaled
    powered = scaled
    for level in range((size_b - 1).bit_length() - 1):
        powered = jnp.dot(powered, powered, precision=highest)
        inverse = jnp.dot(inverse, identity + powered, precision=highest)
    return inverse / half_diag[None, :]


def on_device(matrix, vectors):
    rows_dev, cols_dev = matrix.shape
    row_index = lax.axis_index("row")
    gathered = lax.all_gather(vectors, "col", axis=1, tiled=True)
    row_vectors = mask_vectors(gathered, row_index * rows_dev)
    col_block = lax.axis_index("col") * lax.axis_size("dep") + lax.axis_index("dep")
    offset = col_block * cols_dev - row_index * rows_dev
    local_piece = lax.dynamic_slice_in_dim(row_vectors, offset, cols_dev, 1)
    owner_row = col_block * cols_dev // rows_dev
    col_vectors = broadcast(local_piece, "row", owner_row)
    gram_part = contract(row_vectors, row_vectors, ((1,), (1,)))
    first_part = contract(row_vectors, matrix, ((1,), (0,)))
    gram_total, first_total = lax.psum((gram_part, first_part), "row")
    factor = make_factor(gram_total)
    partial_value = contract(col_vectors, matrix, ((1,), (1,)))
    summed = lax.psum(partial_value, ("col", "dep"))
    update = contract(factor, summed, ((0,), (0,)))
    cross_term = lax.psum(contract(row_vectors, update, ((1,), (1,))), "row")
    left_terms = first_total - jnp.dot(cross_term, col_vectors, precision=highest)
    scaled_terms = contract(factor, left_terms, ((0,), (0,)))
    stacked_left = jnp.concatenate([update, row_vectors], axis=0)
    stacked_right = jnp.concatenate([col_vectors, scaled_terms], axis=0)
    return matrix - contract(stacked_left, stacked_right, ((0,), (0,)))


def solution(mesh):
    placed = (P("row", ("col", "dep")), P(None, ("row", "col")))
    return jax.shard_map(
        on_device, mesh=mesh, in_specs=placed, out_specs=P("row", ("col", "dep")), check_vma=False
    )
```

profile of v0, /device:TPU:6, one launch (start us, length us, event | category | flops | bytes accessed | tf_op | source)
XLA Modules:
  0.0 294.3 jit_solution(16607201885257769943)
XLA Ops:
  6.5 0.0 all-gather.2.cloned.1.call-start
  6.5 0.7 all-gather.2.cloned.1.call-update
  7.3 0.0 all-reduce.6.cloned.1.call-start
  7.4 30.7 %all-gather.2.cloned.1.call-done = f32[64,4096]{1,0:T(8,128)} async-done(((f32[64,1024]{1,0:T(8,128)}), f32[64,4096]{1,0:T(8,128)}) %all-gather.2.cloned.1.call-update) | async-done | bytes 1048592 | tf_op jit(solution)/shard_map/all_gather | solution.py:42
  38.1 1.4 select_select_fusion
  39.5 1.0 fusion.14
  40.5 14.3 %psum.35 = f32[64,64]{1,0:T(8,128)S(1)} all-reduce(f32[64,64]{1,0:T(8,128)S(1)} %fusion.14), channel_id=1, replica_groups=mesh['row'=4,'col'=4,'dep'=2] {'row'}, use_global_device_ids=true, to_apply=%region_0.1 | all-reduce | flops 4096 | bytes 32768 | tf_op jit(solution)/shard_map/psum | solution.py:51
  54.8 0.8 gather_fusion
  55.6 0.2 fusion.10
  55.9 0.2 fusion.15
  56.0 24.8 %fusion.20 = f32[64,2048]{1,0:T(8,128)} fusion(f32[64,4096]{1,0:T(8,128)S(1)} %select_select_fusion, f32[4096,2048]{1,0:T(8,128)} %param.2), kind=kOutput, calls=%fused_computation.39 | convolution fusion | flops 6442450944 | bytes 35127296 | tf_op jit(solution)/shard_map/dot_general | solution.py:15
  80.8 0.8 dynamic-slice_select_fusion
  81.7 0.0 all-reduce.6.cloned.1.call-update
  81.7 0.2 all-reduce.4.cloned.1.call-start
  81.9 0.2 fusion.16
  82.1 0.2 fusion.6
  82.3 0.2 fusion.7
  82.5 0.2 fusion.17
  82.7 0.2 fusion.8
  82.9 50.1 %all-reduce.6.cloned.1.call-done = (f32[64,2048]{1,0:T(8,128)}, f32[64,2048]{1,0:T(8,128)}) async-done(((f32[64,2048]{1,0:T(8,128)}, f32[64,2048]{1,0:T(8,128)}), (f32[64,2048]{1,0:T(8,128)}, f32[64,2048]{1,0:T(8,128)})) %all-reduce.6.cloned.1.call-update) | async-done | bytes 1048592 | tf_op jit(solution)/shard_map/psum | solution.py:11
  133.0 42.8 %fusion.18 = f32[64,4096]{1,0:T(8,128)} fusion(f32[64,2048]{1,0:T(8,128)} %get-tuple-element.5, f32[4096,2048]{1,0:T(8,128)} %param.2), kind=kOutput, calls=%fused_computation.37 | convolution fusion | flops 6442450944 | bytes 35127296 | tf_op jit(solution)/shard_map/dot_general | solution.py:15
  175.8 0.0 all-reduce.4.cloned.1.call-update
  175.8 0.2 convolution_add_fusion
  176.0 0.2 fusion.9
  176.2 0.2 convolution_divide_fusion
  176.3 59.8 %all-reduce.4.cloned.1.call-done = f32[64,4096]{1,0:T(8,128)} async-done(((f32[64,4096]{1,0:T(8,128)}), f32[64,4096]{1,0:T(8,128)}) %all-reduce.4.cloned.1.call-update) | async-done | bytes 1048592 | tf_op jit(solution)/shard_map/psum | solution.py:54
  236.2 2.2 fusion.19
  238.4 1.0 fusion.21
  239.4 14.3 %psum.39 = f32[64,64]{1,0:T(8,128)S(1)} all-reduce(f32[64,64]{1,0:T(8,128)S(1)} %fusion.21), channel_id=1, replica_groups=mesh['row'=4,'col'=4,'dep'=2] {'row'}, use_global_device_ids=true, to_apply=%region_4.5 | all-reduce | flops 4096 | bytes 32768 | tf_op jit(solution)/shard_map/psum | solution.py:56
  253.7 0.6 convolution_subtract_fusion.1
  254.3 0.6 fusion.22
  254.9 32.9 %convolution_subtract_fusion = f32[4096,2048]{1,0:T(8,128)} fusion(f32[4096,2048]{1,0:T(8,128)} %param.2, f32[64,4096]{1,0:T(8,128)S(1)} %select_select_fusion, f32[64,4096]{1,0:T(8,128)S(1)} %fusion.19, f32[64,2048]{1,0:T(8,128)S(1)} %fusion.22, f32[64,2048]{1,0:T(8,128)S(1)} %copy-done), kind=kOutput, calls=%fused_computation.1 | convolution fusion | flops 12894076928 | bytes 70254592 | tf_op jit(solution)/shard_map/dot_general | solution.py:15
  (8 shorter events, 0.0 us)
Async XLA Ops:
  6.5 31.6 %all-gather.2.cloned.1.call-start = ((), (), s32[]{:S(2)}) async-start(), calls=%async_computation | async-start | bytes 1310720 | tf_op jit(solution)/shard_map/all_gather | solution.py:42
  7.3 125.7 %all-reduce.6.cloned.1.call-start = ((), (), s32[]{:S(2)}) async-start(), calls=%async_computation.2 | async-start | bytes 2097152 | tf_op jit(solution)/shard_map/psum | solution.py:11
  81.7 154.5 %all-reduce.4.cloned.1.call-start = ((), (), s32[]{:S(2)}) async-start(), calls=%async_computation.1 | async-start | bytes 2097152 | tf_op jit(solution)/shard_map/psum | solution.py:54
  133.0 120.7 %copy-start = (f32[64,2048]{1,0:T(8,128)S(1)}, f32[64,2048]{1,0:T(8,128)}, u32[]{:S(2)}) copy-start(f32[64,2048]{1,0:T(8,128)} %get-tuple-element.5) | copy-start | bytes 1572868
  133.0 120.8 %copy-start.1 = (f32[64,2048]{1,0:T(8,128)S(1)}, f32[64,2048]{1,0:T(8,128)}, u32[]{:S(2)}) copy-start(f32[64,2048]{1,0:T(8,128)} %get-tuple-element.6) | copy-start | bytes 1572868
Sparse Core Ops, SparseCore 0:
  8.9 29.1 all-gather.1
  81.8 51.0 all-reduce.5
  175.9 60.1 all-reduce.3
where the time goes:
time: 298 us; the launch traced here: 294 us
  waiting for transfers between devices  141 us (47%)
  matrix products  108 us (36%)
  blocking collectives  28.6 us (10%)
  between operations  13.3 us (4%)
    dot_general x7, matrix products, contract(): return lax.dot_general(left, right, (dims, ((), ())), precision=highest)  105 us
    psum x1, waiting for transfers between devices, on_device(): summed = lax.psum(partial_value, ('col', 'dep'))  59.8 us
    psum x1, waiting for transfers between devices, broadcast(): return lax.psum(kept, axis)  50.1 us
    all_gather x1, waiting for transfers between devices, on_device(): gathered = lax.all_gather(vectors, 'col', axis=1, tiled=True)  30.7 us
    psum x1, blocking collectives, on_device(): gram_total, first_total = lax.psum((gram_part, first_part), 'row')  14.3 us
    psum x1, blocking collectives, on_device(): cross_term = lax.psum(contract(row_vectors, update, ((1,), (1,))), 'row')  14.3 us
  transfers between devices with their start and end apart: 3, of which 3 were waited for; matrix products, arithmetic and copies ran while one was open for 0% of the time, Pallas kernels for 0%

commit v1 on v0

v1 whole, which is shorter than its diff:
```python
import functools

import jax
import jax.numpy as jnp
from jax import lax
from jax.experimental import pallas as pl
from jax.experimental.pallas import tpu as pltpu
from jax.sharding import PartitionSpec as P

MESH = pl.DeviceIdType.MESH
highest = lax.Precision.HIGHEST
F32, BF16 = jnp.float32, jnp.bfloat16


def dot(a, b, dims=((1,), (0,)), precision=None):
    return lax.dot_general(a, b, (dims, ((), ())), precision=precision, preferred_element_type=F32)


def split(x):
    hi = x.astype(BF16)
    return hi, (x - hi.astype(F32)).astype(BF16)


def masked(values, first):
    pos = first + lax.broadcasted_iota(jnp.int32, values.shape, 1)
    ref = lax.broadcasted_iota(jnp.int32, values.shape, 0)
    filler = jnp.where(pos == ref + 1, 1.0, 0.0).astype(values.dtype)
    return jnp.where(pos > ref + 1, values, filler)


def make_factor(gram):
    size = gram.shape[0]
    i = lax.broadcasted_iota(jnp.int32, gram.shape, 0)
    j = lax.broadcasted_iota(jnp.int32, gram.shape, 1)
    identity = jnp.where(i == j, 1.0, 0.0).astype(F32)
    diag = gram * identity
    half_col = 0.5 * jnp.sum(diag, axis=1, keepdims=True)
    half_row = 0.5 * jnp.sum(diag, axis=0, keepdims=True)
    scaled = jnp.where(j > i, gram, 0.0) / half_col
    inverse = identity - scaled
    powered = scaled
    for _ in range((size - 1).bit_length() - 1):
        powered = dot(powered, powered, precision=highest)
        inverse = dot(inverse, identity + powered, precision=highest)
    return inverse / half_row


def exchange_kernel(R, C, D, m_ref, v_ref, lhs_ref, rhs_ref, mv, vraw, vrf, vhl, vcraw, vchl, zacc, zpart, zrecv,
                    ztot, ypart, ysib, yfl, yfr, ysr, ysl, yfull, gbuf, wdep, wcol, msem,
                    g_s, g_r, vg_sr, vg_sl, vg_r, vs_s, vs_r, vc_s, vc_r, zs_s, zs_r, za_s, za_r,
                    yb_s, yb_r, yr_s, yr_rl, yr_rr, yg_sr, yg_sl, yg_r, ya_s, ya_r, wd_s, wd_r, wc_s, wc_r):
    r, c, d = lax.axis_index("row"), lax.axis_index("col"), lax.axis_index("dep")
    rows, cols = m_ref.shape
    B = v_ref.shape[0] * v_ref.shape[1]
    rp = v_ref.shape[1]
    W = rows // C
    nb, wb = vcraw.shape[0], vcraw.shape[3]
    U = vc_s.shape[0]
    per_slab = U // (nb * D)
    ur = rp // per_slab

    for b in range(C):
        pltpu.make_async_copy(m_ref.at[pl.ds(b * W, W)], mv.at[pl.ds(b * W, W)], msem.at[b]).start()

    barrier = pltpu.get_barrier_semaphore()
    for axis, me, size in (("row", r, R), ("col", c, C), ("dep", d, D)):
        for k in range(1, size):
            pl.semaphore_signal(barrier, inc=1, device_id={axis: lax.rem(me + k, size)}, device_id_type=MESH)
    pl.semaphore_wait(barrier, R + C + D - 3)

    def rc(src, dst, ssem, rsem, axis, to):
        return pltpu.make_async_remote_copy(src_ref=src, dst_ref=dst, send_sem=ssem, recv_sem=rsem,
                                            device_id={axis: to}, device_id_type=MESH)

    def spread(buf, ssem, rsem, axis, me, size):
        for k in range(1, size):
            rc(buf.at[me], buf.at[me], ssem.at[k - 1], rsem.at[k - 1], axis, lax.rem(me + k, size)).start()

    def spread_wait(buf, ssem, rsem, axis, me, size):
        for k in range(1, size):
            got = buf.at[lax.rem(me + size - k, size)]
            rc(got, got, ssem.at[k - 1], rsem.at[k - 1], axis, lax.rem(me + k, size)).wait()

    def sib(buf, b, ssem, rsem):
        return [rc(buf.at[b, d], buf.at[b, d], ssem.at[k - 1, b], rsem.at[k - 1, b], "dep", lax.rem(d + k, D))
                for k in range(1, D)]

    def line_gather(buf, own, ssr, ssl, rs, sib_s, sib_r, send_own):
        def right(src, b):
            return rc(src, buf.at[b, d], ssr.at[b], rs.at[b], "col", lax.rem(c + 1, C))

        def left(src, b):
            return rc(src, buf.at[b, d], ssl.at[b], rs.at[b], "col", lax.rem(c + C - 1, C))

        @pl.when(c < C - 1)
        def _():
            right(own, c).start()

        @pl.when(c > 0)
        def _():
            left(own, c).start()

        if send_own:
            for cp in sib(buf, c, sib_s, sib_r):
                cp.start()
        for s in range(1, C):
            @pl.when(c - s >= 0)
            def _(s=s):
                b = c - s
                right(buf.at[b, d], b).wait_recv()

                @pl.when(c < C - 1)
                def _():
                    right(buf.at[b, d], b).start()
                for cp in sib(buf, b, sib_s, sib_r):
                    cp.start()

            @pl.when(c + s < C)
            def _(s=s):
                b = c + s
                left(buf.at[b, d], b).wait_recv()

                @pl.when(c > 0)
                def _():
                    left(buf.at[b, d], b).start()
                for cp in sib(buf, b, sib_s, sib_r):
                    cp.start()

        def drain():
            for b in range(C):
                @pl.when((c < C - 1) & (b <= c))
                def _(b=b):
                    right(buf.at[b, d], b).wait_send()

                @pl.when((c > 0) & (b >= c))
                def _(b=b):
                    left(buf.at[b, d], b).wait_send()

        def sib_wait(b):
            for k in range(1, D):
                got = buf.at[b, lax.rem(d + D - k, D)]
                rc(got, got, sib_s.at[k - 1, b], sib_r.at[k - 1, b], "dep", lax.rem(d + k, D)).wait()

        for b in range(C):
            if send_own:
                sib_wait(b)
            else:
                @pl.when(b != c)
                def _(b=b):
                    sib_wait(b)
        return drain

    vraw[c] = v_ref[...]
    vdrain = line_gather(vraw, v_ref.at[d], vg_sr, vg_sl, vg_r, vs_s, vs_r, False)

    colblk = c * D + d
    owner = (colblk * cols) // rows
    off = colblk * cols - owner * rows
    first_blk = off // W
    dist = lax.rem(r - owner + R, R)

    def unit(ref, u):
        slab, part = u // per_slab, u % per_slab
        return ref.at[slab // D, slab % D, pl.ds(part * ur, ur)]

    def vr_unit(u):
        slab, part = u // per_slab, u % per_slab
        if cols >= W:
            return vraw.at[first_blk + slab // D, slab % D, pl.ds(part * ur, ur)]
        return vraw.at[first_blk, slab % D, pl.ds(part * ur, ur), pl.ds(pl.multiple_of(off - first_blk * W, 128), cols)]

    def vc_copy(u, src, slot, delta):
        return rc(src, unit(vcraw, u), vc_s.at[u, slot], vc_r.at[u], "row", lax.rem(owner + delta, R))

    @pl.when(dist == 0)
    def _():
        for u in range(U):
            a = 1 + u % (R - 1)
            own_blk = vr_unit(u)
            vc_copy(u, own_blk, 0, a).start()
        for u in range(U):
            unit(vcraw, u)[...] = vr_unit(u)[...]

    for b in range(C):
        full = masked(vraw[b].reshape(B, W), r * rows + b * W)
        vrf[:, b * W:(b + 1) * W] = full
        hi, lo = split(full)
        vhl[0:B, b * W:(b + 1) * W] = hi
        vhl[B:2 * B, b * W:(b + 1) * W] = lo
    lhs_ref[B:2 * B, :] = vrf[...]
    gbuf[r] = dot(vrf[...], vrf[...], ((1,), (1,)), highest)
    spread(gbuf, g_s, g_r, "row", r, R)

    zacc[...] = jnp.zeros_like(zacc)
    t = min(256, W)
    for b in range(C):
        pltpu.make_async_copy(m_ref.at[pl.ds(b * W, W)], mv.at[pl.ds(b * W, W)], msem.at[b]).wait()

        @pl.loop(0, W // t)
        def _(i, b=b):
            at = pl.multiple_of(b * W + i * t, t)
            hi, lo = split(mv[pl.ds(at, t), :])
            v = vhl[:, pl.ds(at, t)]
            two = dot(v, hi)
            zacc[...] += two[0:B] + two[B:2 * B] + dot(v[0:B], lo)

    zr = B // R
    for i in range(R):
        zpart[i] = zacc[i * zr:(i + 1) * zr, :]
    for k in range(1, R):
        to = lax.rem(r + k, R)
        rc(zpart.at[to], zrecv.at[k - 1], zs_s.at[k - 1], zs_r.at[k - 1], "row", to).start()

    for u in range(U):
        a = 1 + u % (R - 1)

        @pl.when(dist == a)
        def _(u=u, a=a):
            vc_copy(u, unit(vcraw, u), 0, a).wait_recv()
            for k in range(1, R):
                if k != a:
                    vc_copy(u, unit(vcraw, u), k, k).start()
    for u in range(U):
        a = 1 + u % (R - 1)

        @pl.when((dist != 0) & (dist != a))
        def _(u=u, a=a):
            vc_copy(u, unit(vcraw, u), 0, a).wait_recv()
    for i in range(nb):
        full = masked(vcraw[i].reshape(B, wb), colblk * cols + i * wb)
        rhs_ref[0:B, i * wb:(i + 1) * wb] = full
        hi, lo = split(full)
        vchl[0:B, i * wb:(i + 1) * wb] = hi
        vchl[B:2 * B, i * wb:(i + 1) * wb] = lo

    order = sorted(range(C), key=lambda j: -abs(2 * j - (C - 1)))
    for j in order:
        @pl.loop(0, W // t)
        def _(i, j=j):
            hi, lo = split(mv[pl.ds(pl.multiple_of(j * W + i * t, t), t), :])
            v = vchl[...]
            two = dot(v, hi, ((1,), (1,)))
            y = two[0:B] + two[B:2 * B] + dot(v[0:B], lo, ((1,), (1,)))
            ypart[j, :, :, pl.ds(pl.multiple_of(i * t, t), t)] = y.reshape(D, rp, t)
        for k in range(1, D):
            to = lax.rem(d + k, D)
            rc(ypart.at[j, to], ysib.at[k - 1, j], yb_s.at[k - 1, j], yb_r.at[k - 1, j], "dep", to).start()

    for k in range(1, R):
        to = lax.rem(r + k, R)
        rc(zpart.at[to], zrecv.at[k - 1], zs_s.at[k - 1], zs_r.at[k - 1], "row", to).wait()
    total = zpart[r]
    for k in range(1, R):
        total = total + zrecv[k - 1]
    ztot[r] = total
    spread(ztot, za_s, za_r, "row", r, R)

    def ysum(j):
        acc = ypart[j, d]
        for k in range(1, D):
            acc = acc + ysib[k - 1, j]
        return acc

    for j in order:
        for k in range(1, D):
            to = lax.rem(d + k, D)
            rc(ypart.at[j, to], ysib.at[k - 1, j], yb_s.at[k - 1, j], yb_r.at[k - 1, j], "dep", to).wait()

    def red_right(j):
        return rc(ysr.at[j], yfl.at[j], yr_s.at[0, j], yr_rl.at[j], "col", lax.rem(c + 1, C))

    def red_left(j):
        return rc(ysl.at[j], yfr.at[j], yr_s.at[1, j], yr_rr.at[j], "col", lax.rem(c + C - 1, C))

    for s in range(C - 1):
        jr, jl = C - 1 - s, s

        @pl.when(c < jr)
        def _(j=jr):
            @pl.when(c == 0)
            def _():
                ysr[j] = ysum(j)

            @pl.when(c > 0)
            def _():
                red_right(j).wait_recv()
                ysr[j] = ysum(j) + yfl[j]
            red_right(j).start()

        @pl.when(c > jl)
        def _(j=jl):
            @pl.when(c == C - 1)
            def _():
                ysl[j] = ysum(j)

            @pl.when(c < C - 1)
            def _():
                red_left(j).wait_recv()
                ysl[j] = ysum(j) + yfr[j]
            red_left(j).start()

    yfull[c, d] = ysum(c)

    @pl.when(c > 0)
    def _():
        red_right(c).wait_recv()
        yfull[c, d] += yfl[c]

    @pl.when(c < C - 1)
    def _():
        red_left(c).wait_recv()
        yfull[c, d] += yfr[c]

    ydrain = line_gather(yfull, yfull.at[c, d], yg_sr, yg_sl, yg_r, ya_s, ya_r, True)

    spread_wait(gbuf, g_s, g_r, "row", r, R)
    gram = gbuf[0]
    for k in range(1, R):
        gram = gram + gbuf[k]
    factor_t = make_factor(gram).T
    spread_wait(ztot, za_s, za_r, "row", r, R)
    z = ztot[...].reshape(B, cols)
    vc = rhs_ref[0:B, :]
    wdep[d] = dot(z, vc, ((1,), (1,)), highest)
    spread(wdep, wd_s, wd_r, "dep", d, D)
    spread_wait(wdep, wd_s, wd_r, "dep", d, D)
    acc = wdep[0]
    for k in range(1, D):
        acc = acc + wdep[k]
    wcol[c] = acc
    spread(wcol, wc_s, wc_r, "col", c, C)
    for b in range(C):
        lhs_ref[0:B, b * W:(b + 1) * W] = dot(factor_t, yfull[b].reshape(B, W), precision=highest)
    spread_wait(wcol, wc_s, wc_r, "col", c, C)
    acc = wcol[0]
    for k in range(1, C):
        acc = acc + wcol[k]
    cross = dot(acc, factor_t, ((1,), (1,)), highest)
    left = z - dot(cross, vc, precision=highest)
    rhs_ref[B:2 * B, :] = dot(factor_t, left, precision=highest)

    vdrain()
    ydrain()
    for j in range(C):
        @pl.when(c < j)
        def _(j=j):
            red_right(j).wait_send()

        @pl.when(c > j)
        def _(j=j):
            red_left(j).wait_send()
    for u in range(U):
        a = 1 + u % (R - 1)

        @pl.when(dist == 0)
        def _(u=u, a=a):
            vc_copy(u, vr_unit(u), 0, a).wait_send()

        @pl.when(dist == a)
        def _(u=u, a=a):
            for k in range(1, R):
                if k != a:
                    vc_copy(u, unit(vcraw, u), k, k).wait_send()


def update_kernel(m_ref, lhs_ref, rhs_ref, out_ref, stack):
    @pl.when(pl.program_id(0) == 0)
    def _():
        hi, lo = split(rhs_ref[...])
        n = hi.shape[0]
        stack[0:n] = hi
        stack[n:2 * n] = hi
        stack[2 * n:3 * n] = lo

    hi, lo = split(lhs_ref[...].T)
    out_ref[...] = m_ref[...] - dot(jnp.concatenate([hi, lo, hi], axis=1), stack[...])


def solution(mesh):
    R, C, D = mesh.shape["row"], mesh.shape["col"], mesh.shape["dep"]

    def step(matrix, vectors):
        rows, cols = matrix.shape
        B, W = vectors.shape
        rp, zr = B // D, B // R
        nb, wb = max(1, cols // W), min(cols, W)
        ur = min(16, rp)
        units = nb * D * (rp // ur)
        dma, vm = pltpu.SemaphoreType.DMA, pltpu.VMEM
        lhs, rhs = pl.pallas_call(
            functools.partial(exchange_kernel, R, C, D),
            out_shape=(jax.ShapeDtypeStruct((2 * B, rows), F32), jax.ShapeDtypeStruct((2 * B, cols), F32)),
            in_specs=[pl.BlockSpec(memory_space=pl.ANY), pl.BlockSpec(memory_space=vm)],
            out_specs=[pl.BlockSpec(memory_space=vm)] * 2,
            scratch_shapes=[
                vm((rows, cols), F32), vm((C, D, rp, W), F32), vm((B, rows), F32), vm((2 * B, rows), BF16),
                vm((nb, D, rp, wb), F32), vm((2 * B, cols), BF16), vm((B, cols), F32), vm((R, zr, cols), F32),
                vm((R - 1, zr, cols), F32), vm((R, zr, cols), F32), vm((C, D, rp, W), F32),
                vm((D - 1, C, rp, W), F32), vm((C, rp, W), F32), vm((C, rp, W), F32), vm((C, rp, W), F32),
                vm((C, rp, W), F32), vm((C, D, rp, W), F32), vm((R, B, B), F32), vm((D, B, B), F32),
                vm((C, B, B), F32), dma((C,)),
                dma((R - 1,)), dma((R - 1,)), dma((C,)), dma((C,)), dma((C,)), dma((D - 1, C)), dma((D - 1, C)),
                dma((units, R)), dma((units,)), dma((R - 1,)), dma((R - 1,)), dma((R - 1,)), dma((R - 1,)),
                dma((D - 1, C)), dma((D - 1, C)), dma((2, C)), dma((C,)), dma((C,)), dma((C,)), dma((C,)), dma((C,)),
                dma((D - 1, C)), dma((D - 1, C)), dma((D - 1,)), dma((D - 1,)), dma((C - 1,)), dma((C - 1,)),
            ],
            compiler_params=pltpu.CompilerParams(collective_id=0, has_side_effects=True, vmem_limit_bytes=60 * 2**20),
            name="exchange",
        )(matrix, vectors.reshape(D, rp, W))
        rb = min(256, rows)
        return pl.pallas_call(
            update_kernel,
            grid=(rows // rb,),
            out_shape=jax.ShapeDtypeStruct((rows, cols), F32),
            in_specs=[
                pl.BlockSpec((rb, cols), lambda i: (i, 0)),
                pl.BlockSpec((2 * B, rb), lambda i: (0, i)),
                pl.BlockSpec((2 * B, cols), lambda i: (0, 0)),
            ],
            out_specs=pl.BlockSpec((rb, cols), lambda i: (i, 0)),
            scratch_shapes=[vm((6 * B, cols), BF16)],
            compiler_params=pltpu.CompilerParams(vmem_limit_bytes=40 * 2**20),
            name="update",
        )(matrix, lhs, rhs)

    return jax.shard_map(
        step, mesh=mesh, in_specs=(P("row", ("col", "dep")), P(None, ("row", "col"))),
        out_specs=P("row", ("col", "dep")), check_vma=False,
    )
```

time: 298 us -> 134 us (0.45); the launches traced: 294 us -> 134 us
  waiting for transfers between devices: 141 us -> 0 us
  Pallas kernels: 0 us -> 131 us
  matrix products: 108 us -> 0 us
  blocking collectives: 28.6 us -> 0 us
  between operations: 13.3 us -> 0.02 us
    pallas_call x0 -> x2, Pallas kernels: none -> 131 us  [the longest x1 99.1 us: step(): pl.pallas_call(functools.partial(exchange_kernel, R, C, D), out_shape=(ja...]
    psum x2 -> x0, waiting for transfers between devices: 110 us -> none  [the longest x1 59.8 us: on_device(): summed = lax.psum(partial_value, ('col', 'dep'))]
    dot_general x18 -> x0, matrix products: 108 us -> none  [the longest x7 105 us: contract(): return lax.dot_general(left, right, (dims, ((), ())), precision=highest)]
    all_gather x1 -> x0, waiting for transfers between devices: 30.7 us -> none  [on_device(): gathered = lax.all_gather(vectors, 'col', axis=1, tiled=True)]
    psum x2 -> x0, blocking collectives: 28.6 us -> none  [the longest x1 14.3 us: on_device(): gram_total, first_total = lax.psum((gram_part, first_part), 'row')]
  transfers between devices with their start and end apart: 3 -> 0, of which waited for: 3 -> 0; matrix products, arithmetic and copies ran while one was open for 0% -> 0% of each run, Pallas kernels for 0% -> 0%
where the time goes in v1:
time: 134 us
  Pallas kernels  131 us (98%)
  local copies, waits for them, and re-layouts  2.81 us (2%)
    pallas_call x1, Pallas kernels, step(): pl.pallas_call(functools.partial(exchange_kernel, R, C, D), out_shape=(ja...  99.1 us
    pallas_call x1, Pallas kernels, step(): pl.pallas_call(update_kernel, grid=(rows // rb,), out_shape=jax.ShapeDtyp...  31.7 us
    unnamed x4, local copies, waits for them, and re-layouts  2.81 us

profile of v1, /device:TPU:6, one launch (start us, length us, event | category | flops | bytes accessed | tf_op | source)
XLA Modules:
  0.0 133.6 jit_solution(1887613237186750676)
XLA Ops:
  0.0 99.1 %exchange.1 = (f32[128,4096]{1,0:T(8,128)}, f32[128,2048]{1,0:T(8,128)}) custom-call(f32[4096,2048]{1,0:T(8,128)} %m_ref.3, f32[2,32,1024]{2,1,0:T(8,128)} %bitcast.1), custom_call_target="tpu_custom_call" | custom-call | tf_op jit(solution)/shard_map/exchange/pallas_call | solution.py:390
  99.1 0.0 copy-start
  99.1 1.6 %copy-done = f32[128,4096]{1,0:T(8,128)S(1)} copy-done((f32[128,4096]{1,0:T(8,128)S(1)}, f32[128,4096]{1,0:T(8,128)}, u32[]{:S(2)}) %copy-start) | copy-done | bytes 2097176
  100.7 0.0 copy-start.1
  100.7 1.2 copy-done.1
  101.9 31.7 %update.1 = f32[4096,2048]{1,0:T(8,128)} custom-call(f32[4096,2048]{1,0:T(8,128)} %m_ref.3, f32[128,4096]{1,0:T(8,128)S(1)} %copy-done, f32[128,2048]{1,0:T(8,128)S(1)} %copy-done.1), custom_call_target="tpu_custom_call" | custom-call | tf_op jit(solution)/shard_map/update/pallas_call | solution.py:411
Async XLA Ops:
  99.1 1.6 %copy-start = (f32[128,4096]{1,0:T(8,128)S(1)}, f32[128,4096]{1,0:T(8,128)}, u32[]{:S(2)}) copy-start(f32[128,4096]{1,0:T(8,128)} %get-tuple-element.7.lhs_ref) | copy-start | bytes 6291460
  100.7 1.2 copy-start.1

commit v2 on v1

--- a/solution.py
+++ b/solution.py
@@ -204,6 +204,17 @@
             two = dot(v, hi)
             zacc[...] += two[0:B] + two[B:2 * B] + dot(v[0:B], lo)
 
+        if b == C // 2 - 1:
+            for u in range(U):
+                a = 1 + u % (R - 1)
+
+                @pl.when(dist == a)
+                def _(u=u, a=a):
+                    vc_copy(u, unit(vcraw, u), 0, a).wait_recv()
+                    for k in range(1, R):
+                        if k != a:
+                            vc_copy(u, unit(vcraw, u), k, k).start()
+
     zr = B // R
     for i in range(R):
         zpart[i] = zacc[i * zr:(i + 1) * zr, :]
@@ -211,15 +222,6 @@
         to = lax.rem(r + k, R)
         rc(zpart.at[to], zrecv.at[k - 1], zs_s.at[k - 1], zs_r.at[k - 1], "row", to).start()
 
-    for u in range(U):
-        a = 1 + u % (R - 1)
-
-        @pl.when(dist == a)
-        def _(u=u, a=a):
-            vc_copy(u, unit(vcraw, u), 0, a).wait_recv()
-            for k in range(1, R):
-                if k != a:
-                    vc_copy(u, unit(vcraw, u), k, k).start()
     for u in range(U):
         a = 1 + u % (R - 1)
 
@@ -407,7 +409,7 @@
             compiler_params=pltpu.CompilerParams(collective_id=0, has_side_effects=True, vmem_limit_bytes=60 * 2**20),
             name="exchange",
         )(matrix, vectors.reshape(D, rp, W))
-        rb = min(256, rows)
+        rb = min(512, rows)
         return pl.pallas_call(
             update_kernel,
             grid=(rows // rb,),

time: 134 us -> 119 us (0.89)
  Pallas kernels: 131 us -> 116 us
    pallas_call x1, Pallas kernels: 99.1 us -> 89.7 us  [step(): pl.pallas_call(functools.partial(exchange_kernel, R, C, D), out_shape=(ja...]
    pallas_call x1, Pallas kernels: 31.7 us -> 26.3 us  [step(): pl.pallas_call(update_kernel, grid=(rows // rb,), out_shape=jax.ShapeDtyp...]
where the time goes in v2:
time: 119 us
  Pallas kernels  116 us (97%)
  local copies, waits for them, and re-layouts  2.81 us (2%)
    pallas_call x1, Pallas kernels, step(): pl.pallas_call(functools.partial(exchange_kernel, R, C, D), out_shape=(ja...  89.7 us
    pallas_call x1, Pallas kernels, step(): pl.pallas_call(update_kernel, grid=(rows // rb,), out_shape=jax.ShapeDtyp...  26.3 us
    unnamed x4, local copies, waits for them, and re-layouts  2.81 us

profile of v2, /device:TPU:6, one launch (start us, length us, event | category | flops | bytes accessed | tf_op | source)
XLA Modules:
  0.0 118.8 jit_solution(11876906941013171079)
XLA Ops:
  0.0 89.7 %exchange.1 = (f32[128,4096]{1,0:T(8,128)}, f32[128,2048]{1,0:T(8,128)}) custom-call(f32[4096,2048]{1,0:T(8,128)} %m_ref.3, f32[2,32,1024]{2,1,0:T(8,128)} %bitcast.1), custom_call_target="tpu_custom_call" | custom-call | tf_op jit(solution)/shard_map/exchange/pallas_call | solution.py:392
  89.7 0.0 copy-start
  89.7 1.6 %copy-done = f32[128,4096]{1,0:T(8,128)S(1)} copy-done((f32[128,4096]{1,0:T(8,128)S(1)}, f32[128,4096]{1,0:T(8,128)}, u32[]{:S(2)}) %copy-start) | copy-done | bytes 2097176
  91.3 0.0 copy-start.1
  91.3 1.2 %copy-done.1 = f32[128,2048]{1,0:T(8,128)S(1)} copy-done((f32[128,2048]{1,0:T(8,128)S(1)}, f32[128,2048]{1,0:T(8,128)}, u32[]{:S(2)}) %copy-start.1) | copy-done | bytes 1048600
  92.5 26.3 %update.1 = f32[4096,2048]{1,0:T(8,128)} custom-call(f32[4096,2048]{1,0:T(8,128)} %m_ref.3, f32[128,4096]{1,0:T(8,128)S(1)} %copy-done, f32[128,2048]{1,0:T(8,128)S(1)} %copy-done.1), custom_call_target="tpu_custom_call" | custom-call | tf_op jit(solution)/shard_map/update/pallas_call | solution.py:413
Async XLA Ops:
  89.7 1.6 %copy-start = (f32[128,4096]{1,0:T(8,128)S(1)}, f32[128,4096]{1,0:T(8,128)}, u32[]{:S(2)}) copy-start(f32[128,4096]{1,0:T(8,128)} %get-tuple-element.7.lhs_ref) | copy-start | bytes 6291460
  91.3 1.2 %copy-start.1 = (f32[128,2048]{1,0:T(8,128)S(1)}, f32[128,2048]{1,0:T(8,128)}, u32[]{:S(2)}) copy-start(f32[128,2048]{1,0:T(8,128)} %get-tuple-element.8.rhs_ref) | copy-start | bytes 3145732
